TPU v7x, 256 devices: a whole 4x4x8 slice. The times are simulated.
256 devices in a mesh: gx: 128 (over x, y_lo, z, core), gy: 2 (over y_hi).
Axes of the slice: x: 4, y: 4 (y_hi: 2, y_lo: 2; y = y_hi * 2 + y_lo), z: 8, core: 2. Of those that a mesh axis runs over, the one named last changes fastest.
Arguments:
- particles: float32 [64, 2, 512, 1024], P(None, None, 'gx', 'gy'), may hold values from -32 to 32, as said below
- background: float32 [2, 512, 1024], P(None, 'gx', 'gy'), may hold values from -6 to 6
- obs_tile: int32 [128, 256], P('gx', 'gy'), may hold values from 0 to 127
- obs_mask: int32 [16, 128, 256], P(None, 'gx', 'gy'), may hold values 0 or 1
- obs_value: float32 [128, 256], P('gx', 'gy'), may hold values from -6 to 6
- obs_var: float32 [128, 256], P('gx', 'gy'), may hold values from 0.1 to 1
Outputs:
- analysis: float32 [64, 2, 512, 1024], P(None, None, 'gx', 'gy')
Inputs may be any that keep to these rules, and one draw needn't show every extreme that they name: `particles`: each particle is a field of order one to a few. `obs_tile`: an observation's value names tile row t // 128 and tile column t % (128) of its slab.
All inputs are finite; a program needn't handle non-finite values. No bound on the sum of `obs_mask` on one device may be relied on, other than what follows from the above.
Results may differ from a plain program's by a relative error of at most 0.0001.
Values sent between devices are 32-bit elements; how exact they have to be, the bound alone decides.
No kernel may reach another device: no remote copies, remote signals or barrier semaphores. Data moves between devices by JAX's collectives and lax.ppermute only.
A program may use at most 64 MiB of HBM per device.

v0:
```python
import functools

import jax
import jax.numpy as jnp
from jax import lax
from jax.experimental import pallas as pl
from jax.experimental.pallas import tpu as pltpu
from jax.sharding import Mesh
from jax.sharding import PartitionSpec as P

TILE = 4
HALF = TILE // 2
LANES = 128
GX = ("gx_0", "gx_1", "gx_2", "gx_3")
AXES = GX + ("gy",)

prior_weight = 0.05
couple_weight = 0.5
epsilon = 1e-06
highest = lax.Precision.HIGHEST
f32 = jnp.float32
bf16 = jnp.bfloat16


def nn(a, b):
    return lax.dot_general(a, b, (((1,), (0,)), ((), ())), precision=highest, preferred_element_type=f32)


def nt(a, b):
    return lax.dot_general(a, b, (((1,), (1,)), ((), ())), precision=highest, preferred_element_type=f32)


def pieces(a):
    hi = a.astype(bf16)
    rest = a - hi.astype(f32)
    mid = rest.astype(bf16)
    return hi, mid, (rest - mid.astype(f32)).astype(bf16)


def dot_exact(a, table, dims):
    return sum(
        lax.dot_general(part, table, (dims, ((), ())), preferred_element_type=f32)
        for part in pieces(a)[::-1]
    )


def own_table(mask_row, tile, cols):
    pattern = jnp.concatenate(mask_row * (8 // TILE), axis=0)
    full = jnp.concatenate([pattern] * (cols // 8), axis=0)
    which = lax.broadcasted_iota(jnp.int32, (cols, LANES), 0).astype(jnp.int32) // TILE
    return jnp.where(which.astype(f32) == tile, full, 0.0).astype(bf16)


def stored_row(ref, l, r, rows, flip):
    return jnp.where(flip == 1, ref[l, rows - 1 - r : rows - r, :], ref[l, r : r + 1, :])


def pack_kernel(
    geom, part_hbm, back_hbm, tile_hbm, mask_hbm, value_hbm, var_hbm, near_ref, far_ref, edge_ref, table_ref,
    part_ref, back_ref, tile_ref, mask_ref, value_ref, var_ref, sems,
):
    count, layers, rows, cols = geom
    tiles = cols // LANES
    per = layers * rows * tiles
    pairs = (
        (mask_hbm, mask_ref), (tile_hbm, tile_ref), (value_hbm, value_ref), (var_hbm, var_ref),
        (back_hbm, back_ref), (part_hbm, part_ref),
    )
    copies = [pltpu.make_async_copy(src, dst, sems.at[k]) for k, (src, dst) in enumerate(pairs)]
    for copy in copies:
        copy.start()
    flip = lax.axis_index("gx_3")
    lane = lax.broadcasted_iota(jnp.int32, (count, LANES), 1)
    for copy in copies[:5]:
        copy.wait()
    tile = tile_ref[...].astype(f32)
    top = layers * HALF * count + count // tiles
    near_ref[top : top + 8, :] = jnp.zeros((8, cols), f32)
    facts = []
    for r in range(rows):
        source = r + flip * (rows - 1 - 2 * r)
        masks = [mask_ref[source * TILE + c].astype(f32) for c in range(TILE)]
        facts += masks
        table_ref[r * cols : (r + 1) * cols, :] = own_table(masks, tile, cols)
    for k, fact in enumerate(facts + [tile, var_ref[...]]):
        near_ref[top + k // tiles : top + k // tiles + 1, (k % tiles) * LANES : (k % tiles + 1) * LANES] = fact
    copies[5].wait()
    edge = jnp.zeros((count, LANES), f32)
    seen = jnp.zeros((count, LANES), f32)
    for l in range(layers):
        for r in range(rows):
            source = r + flip * (rows - 1 - 2 * r)
            base = (l * rows + r) * 2 * TILE + TILE
            back = stored_row(back_ref, l, r, rows, flip)
            half_ref, start = (near_ref, far_ref)[r // HALF], (l * HALF + r % HALF) * count
            state = []
            for ct in range(tiles):
                cell = part_ref[pl.ds((l * tiles + ct) * rows + source, count, stride=per), :]
                state.append(cell)
                dev = cell - back[:, ct * LANES : (ct + 1) * LANES]
                half_ref[start : start + count, ct * LANES : (ct + 1) * LANES] = dev
                if ct == 0:
                    rolled = pltpu.roll(dev, base, axis=1)
                    edge = jnp.where((lane >= base) & (lane < base + TILE), rolled, edge)
                if ct == tiles - 1:
                    rolled = pltpu.roll(dev, base, axis=1)
                    edge = jnp.where((lane >= base - TILE) & (lane < base), rolled, edge)
            if l == 0:
                table = table_ref[r * cols : (r + 1) * cols, :]
                seen = seen + dot_exact(jnp.concatenate(state, axis=1), table, ((1,), (0,)))
    pull = (0.25 * value_ref[...] - 0.0625 * seen) / var_ref[...]
    for r in range(rows):
        base = (layers * rows + r) * 2 * TILE + TILE
        for start, low in ((0, base), (cols - LANES, base - TILE)):
            table = table_ref[r * cols + start : r * cols + start + LANES, :]
            rolled = pltpu.roll(dot_exact(pull, table, ((1,), (1,))), base, axis=1)
            edge = jnp.where((lane >= low) & (lane < low + TILE), rolled, edge)
    edge_ref[...] = edge
    top = layers * HALF * count
    part = count // tiles
    for ct in range(tiles):
        near_ref[top : top + part, ct * LANES : (ct + 1) * LANES] = pull[ct * part : (ct + 1) * part]


def fetch_main(geom, ref):
    count, layers, _, cols = geom
    tiles = cols // LANES
    top = layers * HALF * count + count // tiles

    def fetch(k):
        return ref[top + k // tiles : top + k // tiles + 1, (k % tiles) * LANES : (k % tiles + 1) * LANES]

    return fetch


def pull_main(geom, ref):
    count, layers, _, cols = geom
    top, tiles = layers * HALF * count, cols // LANES
    part = count // tiles
    return jnp.concatenate([ref[top : top + part, ct * LANES : (ct + 1) * LANES] for ct in range(tiles)], axis=0)


def masks_of(fetch, r):
    return [fetch(r * TILE + c) for c in range(TILE)]


def rows_dot(left, right):
    return lax.dot_general(left, right, (((1,), (1,)), ((), ())), preferred_element_type=f32)


def gram_self(parts):
    hi, mid, lo = (part[...] for part in parts)
    cross = rows_dot(hi, lo)
    total = rows_dot(mid, mid) + (cross + cross.T)
    cross = rows_dot(hi, mid)
    return total + (cross + cross.T) + rows_dot(hi, hi)


def gram_cross(left, right):
    total = 0.0
    for i, j in ((2, 0), (0, 2), (1, 1), (1, 0), (0, 1), (0, 0)):
        total = total + rows_dot(left[i][...], right[j][...])
    return total


def slab_row(halves, count, l, r):
    start = (l * HALF + r % HALF) * count
    return halves[r // HALF][start : start + count, :]


def local_kernel(geom, near_ref, far_ref, table_ref, spread_ref, square_ref, *dev_refs):
    count, layers, rows, cols = geom
    pull = pull_main(geom, near_ref)
    for r in range(rows):
        spread_ref[r * count : (r + 1) * count, :] = dot_exact(
            pull, table_ref[r * cols : (r + 1) * cols, :], ((1,), (1,))
        )
    for l in range(layers):
        for r in range(rows):
            k = l * HALF + r % HALF
            half = dev_refs[3 * (r // HALF) : 3 * (r // HALF) + 3]
            for ref, piece in zip(half, pieces(slab_row((near_ref, far_ref), count, l, r))):
                ref[:, k * cols : (k + 1) * cols] = piece
    square_ref[...] = gram_self(dev_refs[:3]) + gram_self(dev_refs[3:])


def edge_tile(side_ref, slot):
    return pltpu.roll(side_ref[...], LANES - (slot * 2 * TILE + TILE), axis=1)


def smooth(mid, up, down):
    wide = mid.shape[1]
    return 8.0 * mid - (pltpu.roll(mid, 1, axis=1) + pltpu.roll(mid, wide - 1, axis=1) + up + down)


def prior_rows(layers, which, field, store):
    for l in range(layers):
        level = {}
        for r in which:
            for near in (r - 1, r, r + 1):
                if near not in level:
                    level[near] = smooth(field(l, near), field(l, near - 1), field(l, near + 1))
            mine = field(l, r)
            curved = smooth(level[r], level[r - 1], level[r + 1])
            store(l, r, mine, (-prior_weight / 16.0) * (curved + 16.0 * couple_weight * (mine - field(1 - l, r))))


def slab_spread(geom, near_ref, r):
    fetch = fetch_main(geom, near_ref)
    table = own_table(masks_of(fetch, r), fetch(geom[2] * TILE), geom[3])
    return dot_exact(pull_main(geom, near_ref), table, ((1,), (1,)))


def gradient_rows(geom, which, own, other, side_ref, side_other_ref, other_row, spread, out_ref):
    count, layers, rows, _ = geom

    def row_of(r):
        return (own, side_ref, r) if 0 <= r < rows else (other, side_other_ref, other_row(r))

    def field(l, r):
        halves, side, rr = row_of(r)
        return jnp.concatenate([slab_row(halves, count, l, rr), edge_tile(side, l * rows + rr)], axis=1)

    def put(l, r, mine, out):
        if l == 0:
            _, side, rr = row_of(r)
            out = out + jnp.concatenate([spread(r), edge_tile(side, layers * rows + rr)], axis=1)
        start = (l * len(which) + r - which[0]) * count
        out_ref[start : start + count, :] = out

    prior_rows(layers, which, field, put)


def upper_kernel(
    geom, near_ref, far_ref, high_near_ref, high_far_ref, side_ref, side_high_ref, spread_ref, up_ref
):
    count, _, rows, _ = geom
    which = tuple(range(rows - 2, rows + 2))
    own, other = (near_ref, far_ref), (high_near_ref, high_far_ref)
    other_row = lambda r: 2 * rows - 1 - r

    def spread(r):
        if r < rows:
            return spread_ref[r * count : (r + 1) * count, :]
        return slab_spread(geom, high_near_ref, other_row(r))

    gradient_rows(geom, which, own, other, side_ref, side_high_ref, other_row, spread, up_ref)


def gradient_at(count, l, r, down_ref, mid_ref, up_ref):
    if r < 0:
        ref, start = down_ref, (l * 2 + r + 2) * count
    elif r < 2:
        ref, start = mid_ref, (l * 2 + r) * count
    else:
        ref, start = up_ref, (l * 4 + r - 2) * count
    return ref[start : start + count, :]


def linear_rows(geom, which, field, extra, hess_ref, parts):
    count, layers, _, cols = geom

    def put(l, r, mine, out):
        out = out[:, 0:cols]
        if l == 0:
            out = out + extra(r)
        k = l * HALF + r % HALF
        hess_ref[k * count : (k + 1) * count, :] = out
        span = slice(k * cols, (k + 1) * cols)
        for ref, grad, hess in zip(parts, pieces(mine[:, 0:cols]), pieces(out)):
            ref[0:count, span] = grad
            ref[count:, span] = hess

    prior_rows(layers, which, field, put)


def middle_kernel(
    geom, near_ref, far_ref, low_near_ref, side_ref, side_low_ref, spread_ref, up_ref, table_ref,
    dev_hi, dev_mid, dev_lo, mid_ref, grad_near_ref, grad_far_ref, hess_ref, spread_two_ref, spread_low_ref, with_dev_ref,
    self_ref, *parts,
):
    count, layers, rows, cols = geom
    own = (near_ref, far_ref)
    other_row = lambda r: -1 - r
    spread = lambda r: spread_ref[r * count : (r + 1) * count, :]
    gradient_rows(geom, (0, 1), own, (low_near_ref, None), side_ref, side_low_ref, other_row, spread, mid_ref)
    field = lambda l, r: gradient_at(count, l, r, None, mid_ref, up_ref)
    for l in range(layers):
        for r in range(rows):
            start = (l * HALF + r % HALF) * count
            (grad_near_ref, grad_far_ref)[r // HALF][start : start + count, :] = field(l, r)[:, 0:cols]
    table = lambda r: table_ref[r * cols : (r + 1) * cols, :]
    seen = sum(dot_exact(field(0, r)[:, 0:cols], table(r), ((1,), (0,))) for r in range(rows))
    pull = -0.0625 * seen / fetch_main(geom, near_ref)(rows * TILE + 1)
    for r in range(HALF):
        spread_two_ref[r * count : (r + 1) * count, :] = dot_exact(pull, table(r), ((1,), (1,)))
    for r in (-2, -1):
        spread_low_ref[(r + 2) * count : (r + 3) * count, :] = slab_spread(geom, low_near_ref, other_row(r))
    extra = lambda r: dot_exact(pull, table(r), ((1,), (1,)))
    linear_rows(geom, (2, 3), field, extra, hess_ref, parts)
    with_dev_ref[...] = gram_cross(parts, (dev_hi, dev_mid, dev_lo))
    self_ref[...] = gram_self(parts)


def lower_kernel(
    geom, near_ref, far_ref, low_near_ref, low_far_ref, side_ref, side_low_ref, mid_ref, up_ref, spread_two_ref,
    spread_low_ref, square_ref, with_dev_ref, self_ref, dev_hi, dev_mid, dev_lo, hess_ref, mine_ref, other_ref,
    hi_ref, mid_part_ref, lo_ref, down, full,
):
    count, _, _, _ = geom
    own, other = (near_ref, far_ref), (low_near_ref, low_far_ref)
    other_row = lambda r: -1 - r
    spread = lambda r: spread_low_ref[(r + 2) * count : (r + 3) * count, :]
    gradient_rows(geom, (-2, -1), own, other, side_ref, side_low_ref, other_row, spread, down)
    field = lambda l, r: gradient_at(count, l, r, down, mid_ref, up_ref)
    extra = lambda r: spread_two_ref[r * count : (r + 1) * count, :]
    parts = (hi_ref, mid_part_ref, lo_ref)
    linear_rows(geom, (0, 1), field, extra, hess_ref, parts)
    with_dev = gram_cross(parts, (dev_hi, dev_mid, dev_lo)) + with_dev_ref[...]
    total = gram_self(parts) + self_ref[...]
    c = count
    row = lax.broadcasted_iota(jnp.int32, (c, c), 0)
    col = lax.broadcasted_iota(jnp.int32, (c, c), 1)
    eye = jnp.where(row == col, 1.0, 0.0)
    dd = square_ref[...]
    gd, hd = with_dev[0:c], with_dev[c:]
    gg, hg, hh = total[0:c, 0:c], total[c:, 0:c], total[c:, c:]
    h = c // 2
    full[0:c, 0:c] = jnp.where(col >= row, dd, gg)
    full[0:c, c:] = jnp.where(col >= row, hh, hg)
    full[c : c + h, 0:c] = gd[0:h]
    columns = (
        jnp.sum(gg * eye, axis=1, keepdims=True),
        jnp.sum(hg * eye, axis=1, keepdims=True),
        hd[:, 0:1],
        gd[:, 0:1],
    )
    tail = gd[h:]
    for k, column in enumerate(columns):
        for part in range(2):
            tail = jnp.where(col[0:h] == 2 * k + part, column[part * h : (part + 1) * h], tail)
    full[c : c + h, c:] = tail
    flip = lax.axis_index("gx_3")
    half = full.shape[0] // 2
    mine_ref[...] = full[pl.ds(pl.multiple_of(flip * half, 8), half), :]
    other_ref[...] = full[pl.ds(pl.multiple_of((1 - flip) * half, 8), half), :]


def mix_kernel(
    geom, total_size, mine_ref, other_ref, grad_near_ref, grad_far_ref, hess_near_ref, hess_far_ref, part_hbm,
    back_hbm, out_ref, full, part_ref, back_ref, sems,
):
    count, layers, rows, cols = geom
    tiles = cols // LANES
    per = layers * rows * tiles
    copies = [
        pltpu.make_async_copy(part_hbm, part_ref, sems.at[0]),
        pltpu.make_async_copy(back_hbm, back_ref, sems.at[1]),
    ]
    for copy in copies:
        copy.start()
    flip = lax.axis_index("gx_3")
    c = count
    half = mine_ref.shape[0]
    full[pl.ds(pl.multiple_of(flip * half, 8), half), :] = mine_ref[...]
    full[pl.ds(pl.multiple_of((1 - flip) * half, 8), half), :] = other_ref[...]
    row = lax.broadcasted_iota(jnp.int32, (c, c), 0)
    col = lax.broadcasted_iota(jnp.int32, (c, c), 1)
    eye = jnp.where(row == col, 1.0, 0.0)
    pair_count = float(c * (c - 1))
    left, right = full[0:c, 0:c], full[0:c, c:]
    left_t, right_t = left.T, right.T
    h = c // 2
    head, tail = full[c : c + h, 0:c], full[c : c + h, c:]

    def column(k):
        return jnp.concatenate([tail[:, 2 * k : 2 * k + 1], tail[:, 2 * k + 1 : 2 * k + 2]], axis=0)

    dd = jnp.where(col >= row, left, left_t)
    hh = jnp.where(col >= row, right, right_t)
    gg = jnp.where(row > col, left, jnp.where(row < col, left_t, column(0)))
    hg = jnp.where(row > col, right, jnp.where(row < col, right_t, column(1)))
    head_t = jnp.concatenate([head, jnp.zeros((h, c), f32)], axis=0).T
    mirrored = head_t[h:] - (head_t[h:, 0:1] - column(3)[h:]) + (head[0:1] - head_t[0:1])
    gd = jnp.concatenate([head, jnp.where(col[0:h] < h, mirrored, tail)], axis=0)
    hd = gg - (gg[:, 0:1] - column(2))

    def weights(gram):
        distance = (
            jnp.sum(gram * eye, axis=1, keepdims=True) + jnp.sum(gram * eye, axis=0, keepdims=True) - 2.0 * gram
        )
        width = jnp.sum(distance * (1.0 - eye), keepdims=True) / (pair_count * total_size) + epsilon
        kernel = jnp.exp(-distance / (2.0 * width * total_size))
        spread = (eye * jnp.sum(kernel, axis=1, keepdims=True) - kernel) / (width * c)
        return kernel / c, spread

    def step_scale(square_sum):
        return 1.0 / jnp.sqrt(square_sum / (c * total_size) + epsilon)

    push, pull = weights(dd)
    drift_dev = nn(pull, dd) + nn(push, gd)
    drift_grad = nt(pull, gd) + nn(push, gg)
    drift_drift = nt(drift_dev, pull) + nt(drift_grad, push)
    scale = step_scale(jnp.sum(drift_drift * eye, keepdims=True))
    gram = dd + scale * (drift_dev + drift_dev.T) + scale * scale * drift_drift
    push_two, pull_two = weights(gram)
    keep = eye + scale * pull
    gain = scale * push
    on_dev = nn(pull_two, keep)
    on_grad = nn(push_two, keep) + nn(pull_two, gain)
    on_hess = nn(push_two, gain)
    square = jnp.sum(
        nn(on_dev, dd) * on_dev
        + nn(on_grad, gg) * on_grad
        + nn(on_hess, hh) * on_hess
        + 2.0 * (nn(on_grad, gd) * on_dev + nn(on_hess, hd) * on_dev + nn(on_hess, hg) * on_grad),
        keepdims=True,
    )
    scale_two = step_scale(square)
    mix = jnp.concatenate(
        [scale * pull + scale_two * on_dev, gain + scale_two * on_grad, scale_two * on_hess], axis=1
    )
    mix = pieces(mix)
    lefts = (jnp.concatenate(mix, axis=0), jnp.concatenate(mix[:2], axis=0), mix[0])
    for copy in copies:
        copy.wait()
    for l in range(layers):
        for r in range(rows):
            source = r + flip * (rows - 1 - 2 * r)
            places = [pl.ds((l * tiles + ct) * rows + source, c, stride=per) for ct in range(tiles)]
            state = jnp.concatenate([part_ref[place, :] for place in places], axis=1)
            own = state - stored_row(back_ref, l, r, rows, flip)
            grad = slab_row((grad_near_ref, grad_far_ref), c, l, r)
            hess = slab_row((hess_near_ref, hess_far_ref), c, l, r)
            stack = pieces(jnp.concatenate([own, grad, hess], axis=0))
            parts = [
                lax.dot_general(a, b, (((1,), (0,)), ((), ())), preferred_element_type=f32)
                for a, b in zip(lefts, stack)
            ]
            small = parts[0][2 * c :] + parts[1][c:] + parts[2]
            drift = (small + (parts[0][c : 2 * c] + parts[1][0:c])) + parts[0][0:c]
            new = state + drift
            for ct, place in enumerate(places):
                out_ref[place, :] = new[:, ct * LANES : (ct + 1) * LANES]


def all_sum(mine, other):
    swap = [(0, 1), (1, 0)]
    held = mine + lax.ppermute(other, "gx_3", swap)
    for axes in (("gx_2",), ("gx_0", "gx_1", "gy")):
        size = 1
        for axis in axes:
            size *= lax.axis_size(axis)
        copies = jnp.broadcast_to(held, (size,) + held.shape)
        held = jnp.sum(lax.all_to_all(copies, axes, 0, 0, tiled=True), axis=0)
    return held, lax.ppermute(held, "gx_3", swap)


def swapped(count_x, count_y, pair, flip):
    pairs = []
    for x in range(count_x):
        step = 0 if pair is None else (1 if x % 2 == pair else -1)
        target = (x + step) % count_x
        for y in range(count_y):
            pairs.append((x * count_y + y, target * count_y + ((y + 1) % count_y if flip else y)))
    return pairs


def per_device(particles, background, obs_tile, obs_mask, obs_value, obs_var):
    geom = particles.shape
    count, layers, rows, cols = geom
    tiles = cols // LANES
    count_x, count_y = lax.axis_size(GX), lax.axis_size("gy")
    total_size = float(layers * rows * cols * count_x * count_y)
    flat = particles.reshape(count, layers, rows, tiles, LANES).transpose(0, 1, 3, 2, 4)
    flat = flat.reshape(count * layers * rows * tiles, LANES)
    half = layers * HALF * count
    wide = cols + LANES
    params = pltpu.CompilerParams(vmem_limit_bytes=24 * 1024 * 1024)
    shape = jax.ShapeDtypeStruct
    inputs = (flat, background, obs_tile, obs_mask, obs_value, obs_var)
    fixed = [pltpu.with_memory_space_constraint(a, pltpu.HBM) for a in inputs]
    near, far, edge, table = pl.pallas_call(
        functools.partial(pack_kernel, geom),
        out_shape=(
            shape((half + count // tiles + 8, cols), f32),
            shape((half, cols), f32),
            shape((count, LANES), f32),
            shape((rows * cols, LANES), bf16),
        ),
        in_specs=[pl.BlockSpec(memory_space=pltpu.HBM)] * len(inputs),
        scratch_shapes=[pltpu.VMEM(a.shape, a.dtype) for a in inputs] + [pltpu.SemaphoreType.DMA((len(inputs),))],
        compiler_params=params,
        name="pack",
    )(*fixed)

    def send(what, pair, flip):
        return lax.ppermute(what, AXES, swapped(count_x, count_y, pair, flip))

    side = send(edge, None, True)
    low_near = send(near, 1, False)
    side_low = send(side, 1, False)
    low_far = send(far, 1, False)
    high_near = send(near, 0, False)
    high_far = send(far, 0, False)
    side_high = send(side, 0, False)
    piece = shape((count, layers * HALF * cols), bf16)
    spread, square, *dev = pl.pallas_call(
        functools.partial(local_kernel, geom),
        out_shape=(shape((rows * count, cols), f32), shape((count, count), f32)) + (piece,) * 6,
        compiler_params=params,
        name="local",
    )(near, far, table)
    up = pl.pallas_call(
        functools.partial(upper_kernel, geom),
        out_shape=shape((layers * 4 * count, wide), f32),
        compiler_params=params,
        name="upper",
    )(near, far, high_near, high_far, side, side_high, spread)
    parts = [pltpu.VMEM((2 * count, piece.shape[1]), bf16)] * 3
    mid, grad_near, grad_far, hess_far, spread_two, spread_low, with_dev, total = pl.pallas_call(
        functools.partial(middle_kernel, geom),
        out_shape=(
            shape((half, wide), f32),
            shape((half, cols), f32),
            shape((half, cols), f32),
            shape((half, cols), f32),
            shape((HALF * count, cols), f32),
            shape((HALF * count, cols), f32),
            shape((2 * count, count), f32),
            shape((2 * count, 2 * count), f32),
        ),
        scratch_shapes=parts,
        compiler_params=params,
        name="middle",
    )(near, far, low_near, side, side_low, spread, up, table, *dev[3:])
    full = pltpu.VMEM((3 * count // 2, LANES), f32)
    hess_near, mine, other = pl.pallas_call(
        functools.partial(lower_kernel, geom),
        out_shape=(shape((half, cols), f32),) + (shape((3 * count // 4, LANES), f32),) * 2,
        scratch_shapes=parts + [pltpu.VMEM((half, wide), f32), full],
        compiler_params=params,
        name="lower",
    )(near, far, low_near, low_far, side, side_low, mid, up, spread_two, spread_low, square, with_dev, total, *dev[:3])
    mine, other = all_sum(mine, other)
    out = pl.pallas_call(
        functools.partial(mix_kernel, geom, total_size),
        out_shape=shape(flat.shape, f32),
        in_specs=[pl.BlockSpec(memory_space=pltpu.VMEM)] * 6 + [pl.BlockSpec(memory_space=pltpu.HBM)] * 2,
        scratch_shapes=[full, pltpu.VMEM(flat.shape, f32), pltpu.VMEM(background.shape, f32), pltpu.SemaphoreType.DMA((2,))],
        compiler_params=params,
        name="mix",
    )(mine, other, grad_near, grad_far, hess_near, hess_far, *fixed[:2])
    out = out.reshape(count, layers, tiles, rows, LANES).transpose(0, 1, 3, 2, 4)
    return out.reshape(geom)


def solution(mesh):
    count_x = mesh.shape["gx"]
    sizes = (4, 2, 8, 2) if count_x == 128 else (1, 1, count_x // 2, 2)
    finer = Mesh(mesh.devices.reshape(*sizes, mesh.shape["gy"]), AXES)
    in_specs = (
        P(None, None, GX, "gy"),
        P(None, GX, "gy"),
        P(GX, "gy"),
        P(None, GX, "gy"),
        P(GX, "gy"),
        P(GX, "gy"),
    )
    out_specs = P(None, None, GX, "gy")
    return jax.shard_map(per_device, mesh=finer, in_specs=in_specs, out_specs=out_specs, check_vma=False)
```

profile of v0, /device:TPU:1, one launch (start us, length us, event | category | flops | bytes accessed | tf_op | source)
XLA Modules:
  0.0 81.0 jit_solution(11145962356801709368)
XLA Ops:
  0.0 3.0 %pack.1 = (f32[280,512]{1,0:T(8,128)S(1)}, f32[256,512]{1,0:T(8,128)S(1)}, f32[64,128]{1,0:T(8,128)S(1)}, bf16[2048,128]{1,0:T(8,128)(2,1)S(1)}) custom-call(f32[2048,128]{1,0:T(8,128)} %bitcast.10, f32[2,4,512]{2,1,0:T(4,128)} %back_hbm.3, s32[1,128]{1,0:T(1,128)} %tile_hbm.1, s32[16,1,128]{2,1,0:T(1,128)} %mask_hbm.1, f32[1,128]{1,0:T(1,128)} %value_hbm.1, ...), custom_call_target="tpu_custom_call" | custom-call | tf_op jit(solution)/shard_map/pack/pallas_call | solution.py:483
  3.0 3.3 %collective-permute-start.4 = (f32[280,512]{1,0:T(8,128)S(1)}, f32[280,512]{1,0:T(8,128)S(1)}, u32[]{:S(2)}, u32[]{:S(2)}) collective-permute-start(f32[280,512]{1,0:T(8,128)S(1)} %get-tuple-element.28.near_ref), channel_id=1, source_target_pairs={{0,2},{1,3},{2,0},{3,1},{4,6},{5,7},{6,4},{7,5},{8,10},{9,11},{10,... | collective-permute-start | bytes 1720328 | tf_op jit(solution)/shard_map/ppermute | solution.py:498
  6.3 0.0 collective-permute-start
  6.3 7.5 %collective-permute-start.5 = (f32[256,512]{1,0:T(8,128)S(1)}, f32[256,512]{1,0:T(8,128)S(1)}, u32[]{:S(2)}, u32[]{:S(2)}) collective-permute-start(f32[256,512]{1,0:T(8,128)S(1)} %get-tuple-element.29.far_ref), channel_id=1, source_target_pairs={{0,2},{1,3},{2,0},{3,1},{4,6},{5,7},{6,4},{7,5},{8,10},{9,11},{10,... | collective-permute-start | bytes 1572872 | tf_op jit(solution)/shard_map/ppermute | solution.py:498
  13.7 0.0 collective-permute-start.1
  13.8 2.6 %collective-permute-start.2 = (f32[64,128]{1,0:T(8,128)S(1)}, f32[64,128]{1,0:T(8,128)S(1)}, u32[]{:S(2)}, u32[]{:S(2)}) collective-permute-start(f32[64,128]{1,0:T(8,128)S(1)} %get-tuple-element.30), channel_id=1, source_target_pairs={{0,1},{1,0},{2,3},{3,2},{4,5},{5,4},{6,7},{7,6},{8,9},{9,8},{10,11... | collective-permute-start | bytes 98312 | tf_op jit(solution)/shard_map/ppermute | solution.py:498
  16.4 10.0 %collective-permute-done.2.side_ref = f32[64,128]{1,0:T(8,128)S(1)} collective-permute-done((f32[64,128]{1,0:T(8,128)S(1)}, f32[64,128]{1,0:T(8,128)S(1)}, u32[]{:S(2)}, u32[]{:S(2)}) %collective-permute-start.2) | collective-permute-done | bytes 32800 | tf_op jit(solution)/shard_map/ppermute | solution.py:498
  26.4 0.5 collective-permute-start.6
  26.9 0.9 %collective-permute-done.6.side_high_ref = f32[64,128]{1,0:T(8,128)S(1)} collective-permute-done((f32[64,128]{1,0:T(8,128)S(1)}, f32[64,128]{1,0:T(8,128)S(1)}, u32[]{:S(2)}, u32[]{:S(2)}) %collective-permute-start.6) | collective-permute-done | bytes 32800 | tf_op jit(solution)/shard_map/ppermute | solution.py:498
  27.7 0.0 collective-permute-start.3
  27.7 1.3 %local.1 = (f32[256,512]{1,0:T(8,128)S(1)}, f32[64,64]{1,0:T(8,128)S(1)}, bf16[64,2048]{1,0:T(8,128)(2,1)S(1)}, bf16[64,2048]{1,0:T(8,128)(2,1)S(1)}, bf16[64,20...) custom-call(f32[280,512]{1,0:T(8,128)S(1)} %get-tuple-element.28.nea, ...), custom_call_target="tpu_custom_call" | custom-call | tf_op jit(solution)/shard_map/local/pallas_call | solution.py:508
  29.1 0.0 collective-permute-done.5.high_far_ref
  29.1 0.0 collective-permute-done.4.high_near_ref
  29.1 2.7 %upper.1.up_ref = f32[512,640]{1,0:T(8,128)S(1)} custom-call(f32[280,512]{1,0:T(8,128)S(1)} %get-tuple-element.28.near_ref, f32[256,512]{1,0:T(8,128)S(1)} %get-tuple-element.29.far_ref, f32[280,512]{1,0:T(8,128)S(1)} %collective-permute-done.4.high_near_ref, f32[256,512]{1,0:T(8,128)S(1)} %collective-permute-done.5.high_far_ref, ...), custom_call_target="tpu_custom_call" | custom-call | tf_op jit(solution)/shard_map/upper/pallas_call | solution.py:514
  31.8 0.0 collective-permute-done.3.side_low_ref
  31.8 0.0 collective-permute-done.low_near_ref
  31.8 4.1 %middle.1 = (f32[256,640]{1,0:T(8,128)S(1)}, f32[256,512]{1,0:T(8,128)S(1)}, f32[256,512]{1,0:T(8,128)S(1)}, f32[256,512]{1,0:T(8,128)S(1)}, f32[128,512]{1,0:T(...) custom-call(f32[280,512]{1,0:T(8,128)S(1)} %get-tuple-element.28.near_ref, ...), custom_call_target="tpu_custom_call" | custom-call | tf_op jit(solution)/shard_map/middle/pallas_call | solution.py:521
  35.9 0.0 collective-permute-done.1.low_far_ref
  35.9 4.0 %lower.1 = (f32[256,512]{1,0:T(8,128)S(1)}, f32[48,128]{1,0:T(8,128)S(1)}, f32[48,128]{1,0:T(8,128)S(1)}) custom-call(f32[280,512]{1,0:T(8,128)S(1)} %get-tuple-element.28.near_ref, f32[256,512]{1,0:T(8,128)S(1)} %get-tuple-element.29.far_ref, f32[280,512]{1,0:T(8,128)S(1)} %collective-permute-done.low_near_ref, ...), custom_call_target="tpu_custom_call" | custom-call | tf_op jit(solution)/shard_map/lower/pallas_call | solution.py:538
  39.9 6.1 %collective-permute-start.7 = (f32[48,128]{1,0:T(8,128)S(1)}, f32[48,128]{1,0:T(8,128)S(1)}, u32[]{:S(2)}, u32[]{:S(2)}) collective-permute-start(f32[48,128]{1,0:T(8,128)S(1)} %get-tuple-element.46), channel_id=1, source_target_pairs={{0,2},{2,0},{1,3},{3,1},{4,6},{6,4},{5,7},{7,5},{8,10},{10,8},{9,1... | collective-permute-start | bytes 73736 | tf_op jit(solution)/shard_map/ppermute | solution.py:449
  46.0 0.8 %collective-permute-done.7 = f32[48,128]{1,0:T(8,128)S(1)} collective-permute-done((f32[48,128]{1,0:T(8,128)S(1)}, f32[48,128]{1,0:T(8,128)S(1)}, u32[]{:S(2)}, u32[]{:S(2)}) %collective-permute-start.7) | collective-permute-done | bytes 24608 | tf_op jit(solution)/shard_map/ppermute | solution.py:449
  46.8 12.5 %all_to_all.10 = f32[8,48,128]{2,1,0:T(8,128)S(1)} all-to-all(f32[8,48,128]{2,1,0:T(8,128)S(1)} %broadcast_in_dim.6), channel_id=1, replica_groups=mesh['gx_0'=4,'gx_1'=2,'gx_2'=8,'gx_3'=2,'gy'=2] {'gx_2'}, dimensions={0} | all-to-all | bytes 393216 | tf_op jit(solution)/shard_map/all_to_all | solution.py:455
  59.4 11.7 %all_to_all.11 = f32[16,48,128]{2,1,0:T(8,128)S(1)} all-to-all(f32[16,48,128]{2,1,0:T(8,128)S(1)} %broadcast_in_dim.7), channel_id=1, replica_groups=mesh['gx_0'=4,'gx_1'=2,'gx_2'=8,'gx_3'=2,'gy'=2] {'gx_0','gx_1','gy'}, dimensions={0} | all-to-all | bytes 786432 | tf_op jit(solution)/shard_map/all_to_all | solution.py:455
  71.2 3.2 %collective-permute-start.8 = (f32[48,128]{1,0:T(8,128)S(1)}, f32[48,128]{1,0:T(8,128)S(1)}, u32[]{:S(2)}, u32[]{:S(2)}) collective-permute-start(f32[48,128]{1,0:T(8,128)S(1)} %reduce_sum.19.mine_ref), channel_id=1, source_target_pairs={{0,2},{2,0},{1,3},{3,1},{4,6},{6,4},{5,7},{7,5},{8,10},{10,8},{9,1... | collective-permute-start | bytes 73736 | tf_op jit(solution)/shard_map/ppermute | solution.py:456
  74.4 0.8 %collective-permute-done.8.other_ref = f32[48,128]{1,0:T(8,128)S(1)} collective-permute-done((f32[48,128]{1,0:T(8,128)S(1)}, f32[48,128]{1,0:T(8,128)S(1)}, u32[]{:S(2)}, u32[]{:S(2)}) %collective-permute-start.8) | collective-permute-done | bytes 24608 | tf_op jit(solution)/shard_map/ppermute | solution.py:456
  75.3 5.5 %mix.1 = f32[2048,128]{1,0:T(8,128)} custom-call(f32[48,128]{1,0:T(8,128)S(1)} %reduce_sum.19.mine_ref, f32[48,128]{1,0:T(8,128)S(1)} %collective-permute-done.8.other_ref, f32[256,512]{1,0:T(8,128)S(1)} %get-tuple-element.47.grad_near_ref, f32[256,512]{1,0:T(8,128)S(1)} %get-tuple-element.48.grad_far_ref, f32[256,512]{1,0:T(8,128)S(1)} %get-tuple-element.49.hess_near_ref, ...), custom_call_target="tpu_custom_call" | custom-call | tf_op jit(solution)/shard_map/mix/pallas_call | solution.py:546
  (5 shorter events, 0.1 us)
Async XLA Ops:
  3.0 26.1 %collective-permute-start.4 = (f32[280,512]{1,0:T(8,128)S(1)}, f32[280,512]{1,0:T(8,128)S(1)}, u32[]{:S(2)}, u32[]{:S(2)}) collective-permute-start(f32[280,512]{1,0:T(8,128)S(1)} %get-tuple-element.28.near_ref), channel_id=1, source_target_pairs={{0,2},{1,3},{2,0},{3,1},{4,6},{5,7},{6,4},{7,5},{8,10},{9,11},{10,... | collective-permute-start | bytes 1720328 | tf_op jit(solution)/shard_map/ppermute | solution.py:498
  6.3 25.5 %collective-permute-start = (f32[280,512]{1,0:T(8,128)S(1)}, f32[280,512]{1,0:T(8,128)S(1)}, u32[]{:S(2)}, u32[]{:S(2)}) collective-permute-start(f32[280,512]{1,0:T(8,128)S(1)} %get-tuple-element.28.near_ref), channel_id=1, source_target_pairs={{0,254},{1,255},{2,4},{3,5},{4,2},{5,3},{6,8},{7,9},{8,6},{9,7},{1... | collective-permute-start | bytes 1720328 | tf_op jit(solution)/shard_map/ppermute | solution.py:498
  6.3 22.8 %collective-permute-start.5 = (f32[256,512]{1,0:T(8,128)S(1)}, f32[256,512]{1,0:T(8,128)S(1)}, u32[]{:S(2)}, u32[]{:S(2)}) collective-permute-start(f32[256,512]{1,0:T(8,128)S(1)} %get-tuple-element.29.far_ref), channel_id=1, source_target_pairs={{0,2},{1,3},{2,0},{3,1},{4,6},{5,7},{6,4},{7,5},{8,10},{9,11},{10,... | collective-permute-start | bytes 1572872 | tf_op jit(solution)/shard_map/ppermute | solution.py:498
  13.7 22.1 %collective-permute-start.1 = (f32[256,512]{1,0:T(8,128)S(1)}, f32[256,512]{1,0:T(8,128)S(1)}, u32[]{:S(2)}, u32[]{:S(2)}) collective-permute-start(f32[256,512]{1,0:T(8,128)S(1)} %get-tuple-element.29.far_ref), channel_id=1, source_target_pairs={{0,254},{1,255},{2,4},{3,5},{4,2},{5,3},{6,8},{7,9},{8,6},{9,7},{1... | collective-permute-start | bytes 1572872 | tf_op jit(solution)/shard_map/ppermute | solution.py:498
  13.8 12.6 %collective-permute-start.2 = (f32[64,128]{1,0:T(8,128)S(1)}, f32[64,128]{1,0:T(8,128)S(1)}, u32[]{:S(2)}, u32[]{:S(2)}) collective-permute-start(f32[64,128]{1,0:T(8,128)S(1)} %get-tuple-element.30), channel_id=1, source_target_pairs={{0,1},{1,0},{2,3},{3,2},{4,5},{5,4},{6,7},{7,6},{8,9},{9,8},{10,11... | collective-permute-start | bytes 98312 | tf_op jit(solution)/shard_map/ppermute | solution.py:498
  26.4 1.4 %collective-permute-start.6 = (f32[64,128]{1,0:T(8,128)S(1)}, f32[64,128]{1,0:T(8,128)S(1)}, u32[]{:S(2)}, u32[]{:S(2)}) collective-permute-start(f32[64,128]{1,0:T(8,128)S(1)} %collective-permute-done.2.side_ref), channel_id=1, source_target_pairs={{0,2},{1,3},{2,0},{3,1},{4,6},{5,7},{6,4},{7,5},{8,10},{9,11},{10,... | collective-permute-start | bytes 98312 | tf_op jit(solution)/shard_map/ppermute | solution.py:498
  27.7 4.0 %collective-permute-start.3 = (f32[64,128]{1,0:T(8,128)S(1)}, f32[64,128]{1,0:T(8,128)S(1)}, u32[]{:S(2)}, u32[]{:S(2)}) collective-permute-start(f32[64,128]{1,0:T(8,128)S(1)} %collective-permute-done.2.side_ref), channel_id=1, source_target_pairs={{0,254},{1,255},{2,4},{3,5},{4,2},{5,3},{6,8},{7,9},{8,6},{9,7},{1... | collective-permute-start | bytes 98312 | tf_op jit(solution)/shard_map/ppermute | solution.py:498
  39.9 6.9 %collective-permute-start.7 = (f32[48,128]{1,0:T(8,128)S(1)}, f32[48,128]{1,0:T(8,128)S(1)}, u32[]{:S(2)}, u32[]{:S(2)}) collective-permute-start(f32[48,128]{1,0:T(8,128)S(1)} %get-tuple-element.46), channel_id=1, source_target_pairs={{0,2},{2,0},{1,3},{3,1},{4,6},{6,4},{5,7},{7,5},{8,10},{10,8},{9,1... | collective-permute-start | bytes 73736 | tf_op jit(solution)/shard_map/ppermute | solution.py:449
  71.2 4.1 %collective-permute-start.8 = (f32[48,128]{1,0:T(8,128)S(1)}, f32[48,128]{1,0:T(8,128)S(1)}, u32[]{:S(2)}, u32[]{:S(2)}) collective-permute-start(f32[48,128]{1,0:T(8,128)S(1)} %reduce_sum.19.mine_ref), channel_id=1, source_target_pairs={{0,2},{2,0},{1,3},{3,1},{4,6},{6,4},{5,7},{7,5},{8,10},{10,8},{9,1... | collective-permute-start | bytes 73736 | tf_op jit(solution)/shard_map/ppermute | solution.py:456
where the time goes:
time: 81.2 us; the launch traced here: 81 us
  blocking collectives  24.3 us (30%)
  starting transfers between devices  23.2 us (29%)
  Pallas kernels  20.6 us (25%)
  waiting for transfers between devices  12.6 us (16%)
    all_to_all x2, blocking collectives, all_sum(): held = jnp.sum(lax.all_to_all(copies, axes, 0, 0, tiled=True), axis=0)  24.3 us
    ppermute x7, starting transfers between devices, send(): return lax.ppermute(what, AXES, swapped(count_x, count_y, pair, flip))  13.9 us
    ppermute x7, waiting for transfers between devices, send(): return lax.ppermute(what, AXES, swapped(count_x, count_y, pair, flip))  10.9 us
    ppermute x1, starting transfers between devices, all_sum(): held = mine + lax.ppermute(other, 'gx_3', swap)  6.08 us
    pallas_call x1, Pallas kernels, per_device(): pl.pallas_call(functools.partial(mix_kernel, geom, total_size), out_shape...  5.53 us
    pallas_call x1, Pallas kernels, per_device(): pl.pallas_call(functools.partial(middle_kernel, geom), out_shape=(shape((...  4.09 us
    pallas_call x1, Pallas kernels, per_device(): pl.pallas_call(functools.partial(lower_kernel, geom), out_shape=(shape((h...  3.98 us
    ppermute x1, starting transfers between devices, all_sum(): return (held, lax.ppermute(held, 'gx_3', swap))  3.24 us
  transfers between devices with their start and end apart: 9, of which 4 were waited for; matrix products, arithmetic and copies ran while one was open for 0% of the time, Pallas kernels for 10%

commit v1 on v0

--- a/solution.py
+++ b/solution.py
@@ -61,11 +61,13 @@
 ):
     count, layers, rows, cols = geom
     tiles = cols // LANES
-    per = layers * rows * tiles
+    spans = [pl.ds(l * rows * tiles, rows * tiles) for l in range(layers)]
     pairs = (
         (mask_hbm, mask_ref), (tile_hbm, tile_ref), (value_hbm, value_ref), (var_hbm, var_ref),
-        (back_hbm, back_ref), (part_hbm, part_ref),
-    )
+        (back_hbm, back_ref),
+    ) + tuple((part_hbm.at[:, span, :], part_ref.at[:, span, :]) for span in spans)
+    pitch = part_ref.shape[1]
+    lines = part_ref.reshape(count * pitch, LANES)
     copies = [pltpu.make_async_copy(src, dst, sems.at[k]) for k, (src, dst) in enumerate(pairs)]
     for copy in copies:
         copy.start()
@@ -84,10 +86,10 @@
         table_ref[r * cols : (r + 1) * cols, :] = own_table(masks, tile, cols)
     for k, fact in enumerate(facts + [tile, var_ref[...]]):
         near_ref[top + k // tiles : top + k // tiles + 1, (k % tiles) * LANES : (k % tiles + 1) * LANES] = fact
-    copies[5].wait()
     edge = jnp.zeros((count, LANES), f32)
     seen = jnp.zeros((count, LANES), f32)
     for l in range(layers):
+        copies[5 + l].wait()
         for r in range(rows):
             source = r + flip * (rows - 1 - 2 * r)
             base = (l * rows + r) * 2 * TILE + TILE
@@ -95,7 +97,7 @@
             half_ref, start = (near_ref, far_ref)[r // HALF], (l * HALF + r % HALF) * count
             state = []
             for ct in range(tiles):
-                cell = part_ref[pl.ds((l * tiles + ct) * rows + source, count, stride=per), :]
+                cell = lines[pl.ds((l * tiles + ct) * rows + source, count, stride=pitch), :]
                 state.append(cell)
                 dev = cell - back[:, ct * LANES : (ct + 1) * LANES]
                 half_ref[start : start + count, ct * LANES : (ct + 1) * LANES] = dev
@@ -348,13 +350,13 @@
 
 def mix_kernel(
     geom, total_size, mine_ref, other_ref, grad_near_ref, grad_far_ref, hess_near_ref, hess_far_ref, part_hbm,
-    back_hbm, out_ref, full, part_ref, back_ref, sems,
+    back_hbm, out_hbm, full, part_ref, back_ref, dev_hi, dev_mid, dev_lo, rest_hi, rest_mid, rest_lo, sems,
 ):
     count, layers, rows, cols = geom
     tiles = cols // LANES
     per = layers * rows * tiles
     copies = [
-        pltpu.make_async_copy(part_hbm, part_ref, sems.at[0]),
+        pltpu.make_async_copy(part_hbm, part_ref.at[:, 0:per, :], sems.at[0]),
         pltpu.make_async_copy(back_hbm, back_ref, sems.at[1]),
     ]
     for copy in copies:
@@ -364,6 +366,14 @@
     half = mine_ref.shape[0]
     full[pl.ds(pl.multiple_of(flip * half, 8), half), :] = mine_ref[...]
     full[pl.ds(pl.multiple_of((1 - flip) * half, 8), half), :] = other_ref[...]
+    devs, rests = (dev_hi, dev_mid, dev_lo), (rest_hi, rest_mid, rest_lo)
+    halves = (grad_near_ref, grad_far_ref), (hess_near_ref, hess_far_ref)
+    spans = [slice(k * cols, (k + 1) * cols) for k in range(layers * rows)]
+    for l in range(layers):
+        for r in range(rows):
+            for at, half_refs in enumerate(halves):
+                for ref, piece in zip(rests, pieces(slab_row(half_refs, c, l, r))):
+                    ref[at * c : (at + 1) * c, spans[l * rows + r]] = piece
     row = lax.broadcasted_iota(jnp.int32, (c, c), 0)
     col = lax.broadcasted_iota(jnp.int32, (c, c), 1)
     eye = jnp.where(row == col, 1.0, 0.0)
@@ -401,7 +411,19 @@
     drift_dev = nn(pull, dd) + nn(push, gd)
     drift_grad = nt(pull, gd) + nn(push, gg)
     drift_drift = nt(drift_dev, pull) + nt(drift_grad, push)
-    scale = step_scale(jnp.sum(drift_drift * eye, keepdims=True))
+    scale = step_scale(jnp.sum(drift_dev * pull + drift_grad * push, keepdims=True))
+    for copy in copies:
+        copy.wait()
+    pitch = part_ref.shape[1]
+    lines = part_ref.reshape(c * pitch, LANES)
+    for l in range(layers):
+        for r in range(rows):
+            source = r + flip * (rows - 1 - 2 * r)
+            places = [pl.ds((l * tiles + ct) * rows + source, c, stride=pitch) for ct in range(tiles)]
+            state = jnp.concatenate([lines[place, :] for place in places], axis=1)
+            own = state - stored_row(back_ref, l, r, rows, flip)
+            for ref, piece in zip(devs, pieces(own)):
+                ref[:, spans[l * rows + r]] = piece
     gram = dd + scale * (drift_dev + drift_dev.T) + scale * scale * drift_drift
     push_two, pull_two = weights(gram)
     keep = eye + scale * pull
@@ -422,17 +444,14 @@
     )
     mix = pieces(mix)
     lefts = (jnp.concatenate(mix, axis=0), jnp.concatenate(mix[:2], axis=0), mix[0])
-    for copy in copies:
-        copy.wait()
+    results = []
     for l in range(layers):
         for r in range(rows):
             source = r + flip * (rows - 1 - 2 * r)
-            places = [pl.ds((l * tiles + ct) * rows + source, c, stride=per) for ct in range(tiles)]
-            state = jnp.concatenate([part_ref[place, :] for place in places], axis=1)
-            own = state - stored_row(back_ref, l, r, rows, flip)
-            grad = slab_row((grad_near_ref, grad_far_ref), c, l, r)
-            hess = slab_row((hess_near_ref, hess_far_ref), c, l, r)
-            stack = pieces(jnp.concatenate([own, grad, hess], axis=0))
+            places = [pl.ds((l * tiles + ct) * rows + source, c, stride=pitch) for ct in range(tiles)]
+            state = jnp.concatenate([lines[place, :] for place in places], axis=1)
+            span = spans[l * rows + r]
+            stack = [jnp.concatenate([d[:, span], o[:, span]], axis=0) for d, o in zip(devs, rests)]
             parts = [
                 lax.dot_general(a, b, (((1,), (0,)), ((), ())), preferred_element_type=f32)
                 for a, b in zip(lefts, stack)
@@ -441,7 +460,12 @@
             drift = (small + (parts[0][c : 2 * c] + parts[1][0:c])) + parts[0][0:c]
             new = state + drift
             for ct, place in enumerate(places):
-                out_ref[place, :] = new[:, ct * LANES : (ct + 1) * LANES]
+                lines[place, :] = new[:, ct * LANES : (ct + 1) * LANES]
+        span = pl.ds(l * rows * tiles, rows * tiles)
+        results.append(pltpu.make_async_copy(part_ref.at[:, span, :], out_hbm.at[:, span, :], sems.at[2 + l]))
+        results[-1].start()
+    for result in results:
+        result.wait()
 
 
 def all_sum(mine, other):
@@ -473,7 +497,7 @@
     count_x, count_y = lax.axis_size(GX), lax.axis_size("gy")
     total_size = float(layers * rows * cols * count_x * count_y)
     flat = particles.reshape(count, layers, rows, tiles, LANES).transpose(0, 1, 3, 2, 4)
-    flat = flat.reshape(count * layers * rows * tiles, LANES)
+    flat = flat.reshape(count, layers * rows * tiles, LANES)
     half = layers * HALF * count
     wide = cols + LANES
     params = pltpu.CompilerParams(vmem_limit_bytes=24 * 1024 * 1024)
@@ -489,7 +513,9 @@
             shape((rows * cols, LANES), bf16),
         ),
         in_specs=[pl.BlockSpec(memory_space=pltpu.HBM)] * len(inputs),
-        scratch_shapes=[pltpu.VMEM(a.shape, a.dtype) for a in inputs] + [pltpu.SemaphoreType.DMA((len(inputs),))],
+        scratch_shapes=[pltpu.VMEM((count, flat.shape[1] + 8, LANES), f32)]
+        + [pltpu.VMEM(a.shape, a.dtype) for a in inputs[1:]]
+        + [pltpu.SemaphoreType.DMA((len(inputs) + layers - 1,))],
         compiler_params=params,
         name="pack",
     )(*fixed)
@@ -547,7 +573,10 @@
         functools.partial(mix_kernel, geom, total_size),
         out_shape=shape(flat.shape, f32),
         in_specs=[pl.BlockSpec(memory_space=pltpu.VMEM)] * 6 + [pl.BlockSpec(memory_space=pltpu.HBM)] * 2,
-        scratch_shapes=[full, pltpu.VMEM(flat.shape, f32), pltpu.VMEM(background.shape, f32), pltpu.SemaphoreType.DMA((2,))],
+        out_specs=pl.BlockSpec(memory_space=pltpu.HBM),
+        scratch_shapes=[full, pltpu.VMEM((count, flat.shape[1] + 8, LANES), f32), pltpu.VMEM(background.shape, f32)]
+        + [pltpu.VMEM((k * count, layers * rows * cols), bf16) for k in (1, 1, 1, 2, 2, 2)]
+        + [pltpu.SemaphoreType.DMA((2 + layers,))],
         compiler_params=params,
         name="mix",
     )(mine, other, grad_near, grad_far, hess_near, hess_far, *fixed[:2])

time: 81.2 us -> 80.2 us (0.988)
  Pallas kernels: 20.6 us -> 19.6 us
where the time goes in v1:
time: 80.2 us; the launch traced here: 80 us
  blocking collectives  24.3 us (30%)
  starting transfers between devices  23.2 us (29%)
  Pallas kernels  19.6 us (24%)
  waiting for transfers between devices  12.6 us (16%)
    all_to_all x2, blocking collectives, all_sum(): held = jnp.sum(lax.all_to_all(copies, axes, 0, 0, tiled=True), axis=0)  24.3 us
    ppermute x7, starting transfers between devices, send(): return lax.ppermute(what, AXES, swapped(count_x, count_y, pair, flip))  13.9 us
    ppermute x7, waiting for transfers between devices, send(): return lax.ppermute(what, AXES, swapped(count_x, count_y, pair, flip))  10.9 us
    ppermute x1, starting transfers between devices, all_sum(): held = mine + lax.ppermute(other, 'gx_3', swap)  6.08 us
    pallas_call x1, Pallas kernels, per_device(): pl.pallas_call(functools.partial(mix_kernel, geom, total_size), out_shape...  5.2 us
    pallas_call x1, Pallas kernels, per_device(): pl.pallas_call(functools.partial(middle_kernel, geom), out_shape=(shape((...  4.09 us
    pallas_call x1, Pallas kernels, per_device(): pl.pallas_call(functools.partial(lower_kernel, geom), out_shape=(shape((h...  3.98 us
    ppermute x1, starting transfers between devices, all_sum(): return (held, lax.ppermute(held, 'gx_3', swap))  3.24 us
  transfers between devices with their start and end apart: 9, of which 4 were waited for; matrix products, arithmetic and copies ran while one was open for 0% of the time, Pallas kernels for 10%

profile of v1, /device:TPU:1, one launch (start us, length us, event | category | flops | bytes accessed | tf_op | source)
XLA Modules:
  0.0 80.0 jit_solution(18266008139860171301)
XLA Ops:
  0.0 2.3 %pack.1 = (f32[280,512]{1,0:T(8,128)S(1)}, f32[256,512]{1,0:T(8,128)S(1)}, f32[64,128]{1,0:T(8,128)S(1)}, bf16[2048,128]{1,0:T(8,128)(2,1)S(1)}) custom-call(f32[64,32,128]{2,1,0:T(8,128)} %bitcast.10, f32[2,4,512]{2,1,0:T(4,128)} %back_hbm.3, s32[1,128]{1,0:T(1,128)} %tile_hbm.1, s32[16,1,128]{2,1,0:T(1,128)} %mask_hbm.1, f32[1,128]{1,0:T(1,128)} %value_hbm.1, ...), custom_call_target="tpu_custom_call" | custom-call | tf_op jit(solution)/shard_map/pack/pallas_call | solution.py:507
  2.3 3.3 %collective-permute-start.4 = (f32[280,512]{1,0:T(8,128)S(1)}, f32[280,512]{1,0:T(8,128)S(1)}, u32[]{:S(2)}, u32[]{:S(2)}) collective-permute-start(f32[280,512]{1,0:T(8,128)S(1)} %get-tuple-element.28.near_ref), channel_id=1, source_target_pairs={{0,2},{1,3},{2,0},{3,1},{4,6},{5,7},{6,4},{7,5},{8,10},{9,11},{10,... | collective-permute-start | bytes 1720328 | tf_op jit(solution)/shard_map/ppermute | solution.py:524
  5.6 0.0 collective-permute-start
  5.6 7.5 %collective-permute-start.5 = (f32[256,512]{1,0:T(8,128)S(1)}, f32[256,512]{1,0:T(8,128)S(1)}, u32[]{:S(2)}, u32[]{:S(2)}) collective-permute-start(f32[256,512]{1,0:T(8,128)S(1)} %get-tuple-element.29.far_ref), channel_id=1, source_target_pairs={{0,2},{1,3},{2,0},{3,1},{4,6},{5,7},{6,4},{7,5},{8,10},{9,11},{10,... | collective-permute-start | bytes 1572872 | tf_op jit(solution)/shard_map/ppermute | solution.py:524
  13.1 0.0 collective-permute-start.1
  13.1 2.6 %collective-permute-start.2 = (f32[64,128]{1,0:T(8,128)S(1)}, f32[64,128]{1,0:T(8,128)S(1)}, u32[]{:S(2)}, u32[]{:S(2)}) collective-permute-start(f32[64,128]{1,0:T(8,128)S(1)} %get-tuple-element.30), channel_id=1, source_target_pairs={{0,1},{1,0},{2,3},{3,2},{4,5},{5,4},{6,7},{7,6},{8,9},{9,8},{10,11... | collective-permute-start | bytes 98312 | tf_op jit(solution)/shard_map/ppermute | solution.py:524
  15.7 10.0 %collective-permute-done.2.side_ref = f32[64,128]{1,0:T(8,128)S(1)} collective-permute-done((f32[64,128]{1,0:T(8,128)S(1)}, f32[64,128]{1,0:T(8,128)S(1)}, u32[]{:S(2)}, u32[]{:S(2)}) %collective-permute-start.2) | collective-permute-done | bytes 32800 | tf_op jit(solution)/shard_map/ppermute | solution.py:524
  25.7 0.5 collective-permute-start.6
  26.2 0.9 %collective-permute-done.6.side_high_ref = f32[64,128]{1,0:T(8,128)S(1)} collective-permute-done((f32[64,128]{1,0:T(8,128)S(1)}, f32[64,128]{1,0:T(8,128)S(1)}, u32[]{:S(2)}, u32[]{:S(2)}) %collective-permute-start.6) | collective-permute-done | bytes 32800 | tf_op jit(solution)/shard_map/ppermute | solution.py:524
  27.1 0.0 collective-permute-start.3
  27.1 1.3 %local.1 = (f32[256,512]{1,0:T(8,128)S(1)}, f32[64,64]{1,0:T(8,128)S(1)}, bf16[64,2048]{1,0:T(8,128)(2,1)S(1)}, bf16[64,2048]{1,0:T(8,128)(2,1)S(1)}, bf16[64,20...) custom-call(f32[280,512]{1,0:T(8,128)S(1)} %get-tuple-element.28.nea, ...), custom_call_target="tpu_custom_call" | custom-call | tf_op jit(solution)/shard_map/local/pallas_call | solution.py:534
  28.4 0.0 collective-permute-done.5.high_far_ref
  28.4 0.0 collective-permute-done.4.high_near_ref
  28.4 2.7 %upper.1.up_ref = f32[512,640]{1,0:T(8,128)S(1)} custom-call(f32[280,512]{1,0:T(8,128)S(1)} %get-tuple-element.28.near_ref, f32[256,512]{1,0:T(8,128)S(1)} %get-tuple-element.29.far_ref, f32[280,512]{1,0:T(8,128)S(1)} %collective-permute-done.4.high_near_ref, f32[256,512]{1,0:T(8,128)S(1)} %collective-permute-done.5.high_far_ref, ...), custom_call_target="tpu_custom_call" | custom-call | tf_op jit(solution)/shard_map/upper/pallas_call | solution.py:540
  31.1 0.0 collective-permute-done.3.side_low_ref
  31.1 0.0 collective-permute-done.low_near_ref
  31.1 4.1 %middle.1 = (f32[256,640]{1,0:T(8,128)S(1)}, f32[256,512]{1,0:T(8,128)S(1)}, f32[256,512]{1,0:T(8,128)S(1)}, f32[256,512]{1,0:T(8,128)S(1)}, f32[128,512]{1,0:T(...) custom-call(f32[280,512]{1,0:T(8,128)S(1)} %get-tuple-element.28.near_ref, ...), custom_call_target="tpu_custom_call" | custom-call | tf_op jit(solution)/shard_map/middle/pallas_call | solution.py:547
  35.2 0.0 collective-permute-done.1.low_far_ref
  35.2 4.0 %lower.1 = (f32[256,512]{1,0:T(8,128)S(1)}, f32[48,128]{1,0:T(8,128)S(1)}, f32[48,128]{1,0:T(8,128)S(1)}) custom-call(f32[280,512]{1,0:T(8,128)S(1)} %get-tuple-element.28.near_ref, f32[256,512]{1,0:T(8,128)S(1)} %get-tuple-element.29.far_ref, f32[280,512]{1,0:T(8,128)S(1)} %collective-permute-done.low_near_ref, ...), custom_call_target="tpu_custom_call" | custom-call | tf_op jit(solution)/shard_map/lower/pallas_call | solution.py:564
  39.2 6.1 %collective-permute-start.7 = (f32[48,128]{1,0:T(8,128)S(1)}, f32[48,128]{1,0:T(8,128)S(1)}, u32[]{:S(2)}, u32[]{:S(2)}) collective-permute-start(f32[48,128]{1,0:T(8,128)S(1)} %get-tuple-element.46), channel_id=1, source_target_pairs={{0,2},{2,0},{1,3},{3,1},{4,6},{6,4},{5,7},{7,5},{8,10},{10,8},{9,1... | collective-permute-start | bytes 73736 | tf_op jit(solution)/shard_map/ppermute | solution.py:473
  45.3 0.8 %collective-permute-done.7 = f32[48,128]{1,0:T(8,128)S(1)} collective-permute-done((f32[48,128]{1,0:T(8,128)S(1)}, f32[48,128]{1,0:T(8,128)S(1)}, u32[]{:S(2)}, u32[]{:S(2)}) %collective-permute-start.7) | collective-permute-done | bytes 24608 | tf_op jit(solution)/shard_map/ppermute | solution.py:473
  46.2 12.5 %all_to_all.10 = f32[8,48,128]{2,1,0:T(8,128)S(1)} all-to-all(f32[8,48,128]{2,1,0:T(8,128)S(1)} %broadcast_in_dim.6), channel_id=1, replica_groups=mesh['gx_0'=4,'gx_1'=2,'gx_2'=8,'gx_3'=2,'gy'=2] {'gx_2'}, dimensions={0} | all-to-all | bytes 393216 | tf_op jit(solution)/shard_map/all_to_all | solution.py:479
  58.8 11.7 %all_to_all.11 = f32[16,48,128]{2,1,0:T(8,128)S(1)} all-to-all(f32[16,48,128]{2,1,0:T(8,128)S(1)} %broadcast_in_dim.7), channel_id=1, replica_groups=mesh['gx_0'=4,'gx_1'=2,'gx_2'=8,'gx_3'=2,'gy'=2] {'gx_0','gx_1','gy'}, dimensions={0} | all-to-all | bytes 786432 | tf_op jit(solution)/shard_map/all_to_all | solution.py:479
  70.5 3.2 %collective-permute-start.8 = (f32[48,128]{1,0:T(8,128)S(1)}, f32[48,128]{1,0:T(8,128)S(1)}, u32[]{:S(2)}, u32[]{:S(2)}) collective-permute-start(f32[48,128]{1,0:T(8,128)S(1)} %reduce_sum.19.mine_ref), channel_id=1, source_target_pairs={{0,2},{2,0},{1,3},{3,1},{4,6},{6,4},{5,7},{7,5},{8,10},{10,8},{9,1... | collective-permute-start | bytes 73736 | tf_op jit(solution)/shard_map/ppermute | solution.py:480
  73.8 0.8 %collective-permute-done.8.other_ref = f32[48,128]{1,0:T(8,128)S(1)} collective-permute-done((f32[48,128]{1,0:T(8,128)S(1)}, f32[48,128]{1,0:T(8,128)S(1)}, u32[]{:S(2)}, u32[]{:S(2)}) %collective-permute-start.8) | collective-permute-done | bytes 24608 | tf_op jit(solution)/shard_map/ppermute | solution.py:480
  74.6 5.2 %mix.1 = f32[64,32,128]{2,1,0:T(8,128)} custom-call(f32[48,128]{1,0:T(8,128)S(1)} %reduce_sum.19.mine_ref, f32[48,128]{1,0:T(8,128)S(1)} %collective-permute-done.8.other_ref, f32[256,512]{1,0:T(8,128)S(1)} %get-tuple-element.47.grad_near_ref, f32[256,512]{1,0:T(8,128)S(1)} %get-tuple-element.48.grad_far_ref, ...), custom_call_target="tpu_custom_call" | custom-call | tf_op jit(solution)/shard_map/mix/pallas_call | solution.py:572
  (5 shorter events, 0.1 us)
Async XLA Ops:
  2.3 26.1 %collective-permute-start.4 = (f32[280,512]{1,0:T(8,128)S(1)}, f32[280,512]{1,0:T(8,128)S(1)}, u32[]{:S(2)}, u32[]{:S(2)}) collective-permute-start(f32[280,512]{1,0:T(8,128)S(1)} %get-tuple-element.28.near_ref), channel_id=1, source_target_pairs={{0,2},{1,3},{2,0},{3,1},{4,6},{5,7},{6,4},{7,5},{8,10},{9,11},{10,... | collective-permute-start | bytes 1720328 | tf_op jit(solution)/shard_map/ppermute | solution.py:524
  5.6 25.5 %collective-permute-start = (f32[280,512]{1,0:T(8,128)S(1)}, f32[280,512]{1,0:T(8,128)S(1)}, u32[]{:S(2)}, u32[]{:S(2)}) collective-permute-start(f32[280,512]{1,0:T(8,128)S(1)} %get-tuple-element.28.near_ref), channel_id=1, source_target_pairs={{0,254},{1,255},{2,4},{3,5},{4,2},{5,3},{6,8},{7,9},{8,6},{9,7},{1... | collective-permute-start | bytes 1720328 | tf_op jit(solution)/shard_map/ppermute | solution.py:524
  5.6 22.8 %collective-permute-start.5 = (f32[256,512]{1,0:T(8,128)S(1)}, f32[256,512]{1,0:T(8,128)S(1)}, u32[]{:S(2)}, u32[]{:S(2)}) collective-permute-start(f32[256,512]{1,0:T(8,128)S(1)} %get-tuple-element.29.far_ref), channel_id=1, source_target_pairs={{0,2},{1,3},{2,0},{3,1},{4,6},{5,7},{6,4},{7,5},{8,10},{9,11},{10,... | collective-permute-start | bytes 1572872 | tf_op jit(solution)/shard_map/ppermute | solution.py:524
  13.1 22.1 %collective-permute-start.1 = (f32[256,512]{1,0:T(8,128)S(1)}, f32[256,512]{1,0:T(8,128)S(1)}, u32[]{:S(2)}, u32[]{:S(2)}) collective-permute-start(f32[256,512]{1,0:T(8,128)S(1)} %get-tuple-element.29.far_ref), channel_id=1, source_target_pairs={{0,254},{1,255},{2,4},{3,5},{4,2},{5,3},{6,8},{7,9},{8,6},{9,7},{1... | collective-permute-start | bytes 1572872 | tf_op jit(solution)/shard_map/ppermute | solution.py:524
  13.1 12.6 %collective-permute-start.2 = (f32[64,128]{1,0:T(8,128)S(1)}, f32[64,128]{1,0:T(8,128)S(1)}, u32[]{:S(2)}, u32[]{:S(2)}) collective-permute-start(f32[64,128]{1,0:T(8,128)S(1)} %get-tuple-element.30), channel_id=1, source_target_pairs={{0,1},{1,0},{2,3},{3,2},{4,5},{5,4},{6,7},{7,6},{8,9},{9,8},{10,11... | collective-permute-start | bytes 98312 | tf_op jit(solution)/shard_map/ppermute | solution.py:524
  25.7 1.4 %collective-permute-start.6 = (f32[64,128]{1,0:T(8,128)S(1)}, f32[64,128]{1,0:T(8,128)S(1)}, u32[]{:S(2)}, u32[]{:S(2)}) collective-permute-start(f32[64,128]{1,0:T(8,128)S(1)} %collective-permute-done.2.side_ref), channel_id=1, source_target_pairs={{0,2},{1,3},{2,0},{3,1},{4,6},{5,7},{6,4},{7,5},{8,10},{9,11},{10,... | collective-permute-start | bytes 98312 | tf_op jit(solution)/shard_map/ppermute | solution.py:524
  27.1 4.0 %collective-permute-start.3 = (f32[64,128]{1,0:T(8,128)S(1)}, f32[64,128]{1,0:T(8,128)S(1)}, u32[]{:S(2)}, u32[]{:S(2)}) collective-permute-start(f32[64,128]{1,0:T(8,128)S(1)} %collective-permute-done.2.side_ref), channel_id=1, source_target_pairs={{0,254},{1,255},{2,4},{3,5},{4,2},{5,3},{6,8},{7,9},{8,6},{9,7},{1... | collective-permute-start | bytes 98312 | tf_op jit(solution)/shard_map/ppermute | solution.py:524
  39.2 6.9 %collective-permute-start.7 = (f32[48,128]{1,0:T(8,128)S(1)}, f32[48,128]{1,0:T(8,128)S(1)}, u32[]{:S(2)}, u32[]{:S(2)}) collective-permute-start(f32[48,128]{1,0:T(8,128)S(1)} %get-tuple-element.46), channel_id=1, source_target_pairs={{0,2},{2,0},{1,3},{3,1},{4,6},{6,4},{5,7},{7,5},{8,10},{10,8},{9,1... | collective-permute-start | bytes 73736 | tf_op jit(solution)/shard_map/ppermute | solution.py:473
  70.5 4.1 %collective-permute-start.8 = (f32[48,128]{1,0:T(8,128)S(1)}, f32[48,128]{1,0:T(8,128)S(1)}, u32[]{:S(2)}, u32[]{:S(2)}) collective-permute-start(f32[48,128]{1,0:T(8,128)S(1)} %reduce_sum.19.mine_ref), channel_id=1, source_target_pairs={{0,2},{2,0},{1,3},{3,1},{4,6},{6,4},{5,7},{7,5},{8,10},{10,8},{9,1... | collective-permute-start | bytes 73736 | tf_op jit(solution)/shard_map/ppermute | solution.py:480

commit v2 on v1

--- a/solution.py
+++ b/solution.py
@@ -350,7 +350,7 @@
 
 def mix_kernel(
     geom, total_size, mine_ref, other_ref, grad_near_ref, grad_far_ref, hess_near_ref, hess_far_ref, part_hbm,
-    back_hbm, out_hbm, full, part_ref, back_ref, dev_hi, dev_mid, dev_lo, rest_hi, rest_mid, rest_lo, sems,
+    back_hbm, out_hbm, full, part_ref, back_ref, sems,
 ):
     count, layers, rows, cols = geom
     tiles = cols // LANES
@@ -366,14 +366,6 @@
     half = mine_ref.shape[0]
     full[pl.ds(pl.multiple_of(flip * half, 8), half), :] = mine_ref[...]
     full[pl.ds(pl.multiple_of((1 - flip) * half, 8), half), :] = other_ref[...]
-    devs, rests = (dev_hi, dev_mid, dev_lo), (rest_hi, rest_mid, rest_lo)
-    halves = (grad_near_ref, grad_far_ref), (hess_near_ref, hess_far_ref)
-    spans = [slice(k * cols, (k + 1) * cols) for k in range(layers * rows)]
-    for l in range(layers):
-        for r in range(rows):
-            for at, half_refs in enumerate(halves):
-                for ref, piece in zip(rests, pieces(slab_row(half_refs, c, l, r))):
-                    ref[at * c : (at + 1) * c, spans[l * rows + r]] = piece
     row = lax.broadcasted_iota(jnp.int32, (c, c), 0)
     col = lax.broadcasted_iota(jnp.int32, (c, c), 1)
     eye = jnp.where(row == col, 1.0, 0.0)
@@ -411,19 +403,7 @@
     drift_dev = nn(pull, dd) + nn(push, gd)
     drift_grad = nt(pull, gd) + nn(push, gg)
     drift_drift = nt(drift_dev, pull) + nt(drift_grad, push)
-    scale = step_scale(jnp.sum(drift_dev * pull + drift_grad * push, keepdims=True))
-    for copy in copies:
-        copy.wait()
-    pitch = part_ref.shape[1]
-    lines = part_ref.reshape(c * pitch, LANES)
-    for l in range(layers):
-        for r in range(rows):
-            source = r + flip * (rows - 1 - 2 * r)
-            places = [pl.ds((l * tiles + ct) * rows + source, c, stride=pitch) for ct in range(tiles)]
-            state = jnp.concatenate([lines[place, :] for place in places], axis=1)
-            own = state - stored_row(back_ref, l, r, rows, flip)
-            for ref, piece in zip(devs, pieces(own)):
-                ref[:, spans[l * rows + r]] = piece
+    scale = step_scale(jnp.sum(drift_drift * eye, keepdims=True))
     gram = dd + scale * (drift_dev + drift_dev.T) + scale * scale * drift_drift
     push_two, pull_two = weights(gram)
     keep = eye + scale * pull
@@ -444,14 +424,20 @@
     )
     mix = pieces(mix)
     lefts = (jnp.concatenate(mix, axis=0), jnp.concatenate(mix[:2], axis=0), mix[0])
+    for copy in copies:
+        copy.wait()
+    pitch = part_ref.shape[1]
+    lines = part_ref.reshape(c * pitch, LANES)
     results = []
     for l in range(layers):
         for r in range(rows):
             source = r + flip * (rows - 1 - 2 * r)
             places = [pl.ds((l * tiles + ct) * rows + source, c, stride=pitch) for ct in range(tiles)]
             state = jnp.concatenate([lines[place, :] for place in places], axis=1)
-            span = spans[l * rows + r]
-            stack = [jnp.concatenate([d[:, span], o[:, span]], axis=0) for d, o in zip(devs, rests)]
+            own = state - stored_row(back_ref, l, r, rows, flip)
+            grad = slab_row((grad_near_ref, grad_far_ref), c, l, r)
+            hess = slab_row((hess_near_ref, hess_far_ref), c, l, r)
+            stack = pieces(jnp.concatenate([own, grad, hess], axis=0))
             parts = [
                 lax.dot_general(a, b, (((1,), (0,)), ((), ())), preferred_element_type=f32)
                 for a, b in zip(lefts, stack)
@@ -575,7 +561,6 @@
         in_specs=[pl.BlockSpec(memory_space=pltpu.VMEM)] * 6 + [pl.BlockSpec(memory_space=pltpu.HBM)] * 2,
         out_specs=pl.BlockSpec(memory_space=pltpu.HBM),
         scratch_shapes=[full, pltpu.VMEM((count, flat.shape[1] + 8, LANES), f32), pltpu.VMEM(background.shape, f32)]
-        + [pltpu.VMEM((k * count, layers * rows * cols), bf16) for k in (1, 1, 1, 2, 2, 2)]
         + [pltpu.SemaphoreType.DMA((2 + layers,))],
         compiler_params=params,
         name="mix",

time: 80.2 us -> 80.3 us (level)
  no operation moved by 1% of the time
where the time goes in v2:
time: 80.3 us; the launch traced here: 80.1 us
  blocking collectives  24.3 us (30%)
  starting transfers between devices  23.2 us (29%)
  Pallas kernels  19.7 us (25%)
  waiting for transfers between devices  12.6 us (16%)
    all_to_all x2, blocking collectives, all_sum(): held = jnp.sum(lax.all_to_all(copies, axes, 0, 0, tiled=True), axis=0)  24.3 us
    ppermute x7, starting transfers between devices, send(): return lax.ppermute(what, AXES, swapped(count_x, count_y, pair, flip))  13.9 us
    ppermute x7, waiting for transfers between devices, send(): return lax.ppermute(what, AXES, swapped(count_x, count_y, pair, flip))  10.9 us
    ppermute x1, starting transfers between devices, all_sum(): held = mine + lax.ppermute(other, 'gx_3', swap)  6.08 us
    pallas_call x1, Pallas kernels, per_device(): pl.pallas_call(functools.partial(mix_kernel, geom, total_size), out_shape...  5.32 us
    pallas_call x1, Pallas kernels, per_device(): pl.pallas_call(functools.partial(middle_kernel, geom), out_shape=(shape((...  4.09 us
    pallas_call x1, Pallas kernels, per_device(): pl.pallas_call(functools.partial(lower_kernel, geom), out_shape=(shape((h...  3.98 us
    ppermute x1, starting transfers between devices, all_sum(): return (held, lax.ppermute(held, 'gx_3', swap))  3.24 us
  transfers between devices with their start and end apart: 9, of which 4 were waited for; matrix products, arithmetic and copies ran while one was open for 0% of the time, Pallas kernels for 10%

profile of v2, /device:TPU:1, one launch (start us, length us, event | category | flops | bytes accessed | tf_op | source)
XLA Modules:
  0.0 80.1 jit_solution(4534109132611484436)
XLA Ops:
  0.0 2.3 %pack.1 = (f32[280,512]{1,0:T(8,128)S(1)}, f32[256,512]{1,0:T(8,128)S(1)}, f32[64,128]{1,0:T(8,128)S(1)}, bf16[2048,128]{1,0:T(8,128)(2,1)S(1)}) custom-call(f32[64,32,128]{2,1,0:T(8,128)} %bitcast.10, f32[2,4,512]{2,1,0:T(4,128)} %back_hbm.3, s32[1,128]{1,0:T(1,128)} %tile_hbm.1, s32[16,1,128]{2,1,0:T(1,128)} %mask_hbm.1, f32[1,128]{1,0:T(1,128)} %value_hbm.1, ...), custom_call_target="tpu_custom_call" | custom-call | tf_op jit(solution)/shard_map/pack/pallas_call | solution.py:493
  2.3 3.3 %collective-permute-start.4 = (f32[280,512]{1,0:T(8,128)S(1)}, f32[280,512]{1,0:T(8,128)S(1)}, u32[]{:S(2)}, u32[]{:S(2)}) collective-permute-start(f32[280,512]{1,0:T(8,128)S(1)} %get-tuple-element.28.near_ref), channel_id=1, source_target_pairs={{0,2},{1,3},{2,0},{3,1},{4,6},{5,7},{6,4},{7,5},{8,10},{9,11},{10,... | collective-permute-start | bytes 1720328 | tf_op jit(solution)/shard_map/ppermute | solution.py:510
  5.6 0.0 collective-permute-start
  5.6 7.5 %collective-permute-start.5 = (f32[256,512]{1,0:T(8,128)S(1)}, f32[256,512]{1,0:T(8,128)S(1)}, u32[]{:S(2)}, u32[]{:S(2)}) collective-permute-start(f32[256,512]{1,0:T(8,128)S(1)} %get-tuple-element.29.far_ref), channel_id=1, source_target_pairs={{0,2},{1,3},{2,0},{3,1},{4,6},{5,7},{6,4},{7,5},{8,10},{9,11},{10,... | collective-permute-start | bytes 1572872 | tf_op jit(solution)/shard_map/ppermute | solution.py:510
  13.1 0.0 collective-permute-start.1
  13.1 2.6 %collective-permute-start.2 = (f32[64,128]{1,0:T(8,128)S(1)}, f32[64,128]{1,0:T(8,128)S(1)}, u32[]{:S(2)}, u32[]{:S(2)}) collective-permute-start(f32[64,128]{1,0:T(8,128)S(1)} %get-tuple-element.30), channel_id=1, source_target_pairs={{0,1},{1,0},{2,3},{3,2},{4,5},{5,4},{6,7},{7,6},{8,9},{9,8},{10,11... | collective-permute-start | bytes 98312 | tf_op jit(solution)/shard_map/ppermute | solution.py:510
  15.7 10.0 %collective-permute-done.2.side_ref = f32[64,128]{1,0:T(8,128)S(1)} collective-permute-done((f32[64,128]{1,0:T(8,128)S(1)}, f32[64,128]{1,0:T(8,128)S(1)}, u32[]{:S(2)}, u32[]{:S(2)}) %collective-permute-start.2) | collective-permute-done | bytes 32800 | tf_op jit(solution)/shard_map/ppermute | solution.py:510
  25.7 0.5 collective-permute-start.6
  26.2 0.9 %collective-permute-done.6.side_high_ref = f32[64,128]{1,0:T(8,128)S(1)} collective-permute-done((f32[64,128]{1,0:T(8,128)S(1)}, f32[64,128]{1,0:T(8,128)S(1)}, u32[]{:S(2)}, u32[]{:S(2)}) %collective-permute-start.6) | collective-permute-done | bytes 32800 | tf_op jit(solution)/shard_map/ppermute | solution.py:510
  27.1 0.0 collective-permute-start.3
  27.1 1.3 %local.1 = (f32[256,512]{1,0:T(8,128)S(1)}, f32[64,64]{1,0:T(8,128)S(1)}, bf16[64,2048]{1,0:T(8,128)(2,1)S(1)}, bf16[64,2048]{1,0:T(8,128)(2,1)S(1)}, bf16[64,20...) custom-call(f32[280,512]{1,0:T(8,128)S(1)} %get-tuple-element.28.nea, ...), custom_call_target="tpu_custom_call" | custom-call | tf_op jit(solution)/shard_map/local/pallas_call | solution.py:520
  28.4 0.0 collective-permute-done.5.high_far_ref
  28.4 0.0 collective-permute-done.4.high_near_ref
  28.4 2.7 %upper.1.up_ref = f32[512,640]{1,0:T(8,128)S(1)} custom-call(f32[280,512]{1,0:T(8,128)S(1)} %get-tuple-element.28.near_ref, f32[256,512]{1,0:T(8,128)S(1)} %get-tuple-element.29.far_ref, f32[280,512]{1,0:T(8,128)S(1)} %collective-permute-done.4.high_near_ref, f32[256,512]{1,0:T(8,128)S(1)} %collective-permute-done.5.high_far_ref, ...), custom_call_target="tpu_custom_call" | custom-call | tf_op jit(solution)/shard_map/upper/pallas_call | solution.py:526
  31.1 0.0 collective-permute-done.3.side_low_ref
  31.1 0.0 collective-permute-done.low_near_ref
  31.1 4.1 %middle.1 = (f32[256,640]{1,0:T(8,128)S(1)}, f32[256,512]{1,0:T(8,128)S(1)}, f32[256,512]{1,0:T(8,128)S(1)}, f32[256,512]{1,0:T(8,128)S(1)}, f32[128,512]{1,0:T(...) custom-call(f32[280,512]{1,0:T(8,128)S(1)} %get-tuple-element.28.near_ref, ...), custom_call_target="tpu_custom_call" | custom-call | tf_op jit(solution)/shard_map/middle/pallas_call | solution.py:533
  35.2 0.0 collective-permute-done.1.low_far_ref
  35.2 4.0 %lower.1 = (f32[256,512]{1,0:T(8,128)S(1)}, f32[48,128]{1,0:T(8,128)S(1)}, f32[48,128]{1,0:T(8,128)S(1)}) custom-call(f32[280,512]{1,0:T(8,128)S(1)} %get-tuple-element.28.near_ref, f32[256,512]{1,0:T(8,128)S(1)} %get-tuple-element.29.far_ref, f32[280,512]{1,0:T(8,128)S(1)} %collective-permute-done.low_near_ref, ...), custom_call_target="tpu_custom_call" | custom-call | tf_op jit(solution)/shard_map/lower/pallas_call | solution.py:550
  39.2 6.1 %collective-permute-start.7 = (f32[48,128]{1,0:T(8,128)S(1)}, f32[48,128]{1,0:T(8,128)S(1)}, u32[]{:S(2)}, u32[]{:S(2)}) collective-permute-start(f32[48,128]{1,0:T(8,128)S(1)} %get-tuple-element.46), channel_id=1, source_target_pairs={{0,2},{2,0},{1,3},{3,1},{4,6},{6,4},{5,7},{7,5},{8,10},{10,8},{9,1... | collective-permute-start | bytes 73736 | tf_op jit(solution)/shard_map/ppermute | solution.py:459
  45.3 0.8 %collective-permute-done.7 = f32[48,128]{1,0:T(8,128)S(1)} collective-permute-done((f32[48,128]{1,0:T(8,128)S(1)}, f32[48,128]{1,0:T(8,128)S(1)}, u32[]{:S(2)}, u32[]{:S(2)}) %collective-permute-start.7) | collective-permute-done | bytes 24608 | tf_op jit(solution)/shard_map/ppermute | solution.py:459
  46.2 12.5 %all_to_all.10 = f32[8,48,128]{2,1,0:T(8,128)S(1)} all-to-all(f32[8,48,128]{2,1,0:T(8,128)S(1)} %broadcast_in_dim.6), channel_id=1, replica_groups=mesh['gx_0'=4,'gx_1'=2,'gx_2'=8,'gx_3'=2,'gy'=2] {'gx_2'}, dimensions={0} | all-to-all | bytes 393216 | tf_op jit(solution)/shard_map/all_to_all | solution.py:465
  58.8 11.7 %all_to_all.11 = f32[16,48,128]{2,1,0:T(8,128)S(1)} all-to-all(f32[16,48,128]{2,1,0:T(8,128)S(1)} %broadcast_in_dim.7), channel_id=1, replica_groups=mesh['gx_0'=4,'gx_1'=2,'gx_2'=8,'gx_3'=2,'gy'=2] {'gx_0','gx_1','gy'}, dimensions={0} | all-to-all | bytes 786432 | tf_op jit(solution)/shard_map/all_to_all | solution.py:465
  70.5 3.2 %collective-permute-start.8 = (f32[48,128]{1,0:T(8,128)S(1)}, f32[48,128]{1,0:T(8,128)S(1)}, u32[]{:S(2)}, u32[]{:S(2)}) collective-permute-start(f32[48,128]{1,0:T(8,128)S(1)} %reduce_sum.19.mine_ref), channel_id=1, source_target_pairs={{0,2},{2,0},{1,3},{3,1},{4,6},{6,4},{5,7},{7,5},{8,10},{10,8},{9,1... | collective-permute-start | bytes 73736 | tf_op jit(solution)/shard_map/ppermute | solution.py:466
  73.8 0.8 %collective-permute-done.8.other_ref = f32[48,128]{1,0:T(8,128)S(1)} collective-permute-done((f32[48,128]{1,0:T(8,128)S(1)}, f32[48,128]{1,0:T(8,128)S(1)}, u32[]{:S(2)}, u32[]{:S(2)}) %collective-permute-start.8) | collective-permute-done | bytes 24608 | tf_op jit(solution)/shard_map/ppermute | solution.py:466
  74.6 5.3 %mix.1 = f32[64,32,128]{2,1,0:T(8,128)} custom-call(f32[48,128]{1,0:T(8,128)S(1)} %reduce_sum.19.mine_ref, f32[48,128]{1,0:T(8,128)S(1)} %collective-permute-done.8.other_ref, f32[256,512]{1,0:T(8,128)S(1)} %get-tuple-element.47.grad_near_ref, f32[256,512]{1,0:T(8,128)S(1)} %get-tuple-element.48.grad_far_ref, ...), custom_call_target="tpu_custom_call" | custom-call | tf_op jit(solution)/shard_map/mix/pallas_call | solution.py:558
  (5 shorter events, 0.1 us)
Async XLA Ops:
  2.3 26.1 %collective-permute-start.4 = (f32[280,512]{1,0:T(8,128)S(1)}, f32[280,512]{1,0:T(8,128)S(1)}, u32[]{:S(2)}, u32[]{:S(2)}) collective-permute-start(f32[280,512]{1,0:T(8,128)S(1)} %get-tuple-element.28.near_ref), channel_id=1, source_target_pairs={{0,2},{1,3},{2,0},{3,1},{4,6},{5,7},{6,4},{7,5},{8,10},{9,11},{10,... | collective-permute-start | bytes 1720328 | tf_op jit(solution)/shard_map/ppermute | solution.py:510
  5.6 25.5 %collective-permute-start = (f32[280,512]{1,0:T(8,128)S(1)}, f32[280,512]{1,0:T(8,128)S(1)}, u32[]{:S(2)}, u32[]{:S(2)}) collective-permute-start(f32[280,512]{1,0:T(8,128)S(1)} %get-tuple-element.28.near_ref), channel_id=1, source_target_pairs={{0,254},{1,255},{2,4},{3,5},{4,2},{5,3},{6,8},{7,9},{8,6},{9,7},{1... | collective-permute-start | bytes 1720328 | tf_op jit(solution)/shard_map/ppermute | solution.py:510
  5.6 22.8 %collective-permute-start.5 = (f32[256,512]{1,0:T(8,128)S(1)}, f32[256,512]{1,0:T(8,128)S(1)}, u32[]{:S(2)}, u32[]{:S(2)}) collective-permute-start(f32[256,512]{1,0:T(8,128)S(1)} %get-tuple-element.29.far_ref), channel_id=1, source_target_pairs={{0,2},{1,3},{2,0},{3,1},{4,6},{5,7},{6,4},{7,5},{8,10},{9,11},{10,... | collective-permute-start | bytes 1572872 | tf_op jit(solution)/shard_map/ppermute | solution.py:510
  13.1 22.1 %collective-permute-start.1 = (f32[256,512]{1,0:T(8,128)S(1)}, f32[256,512]{1,0:T(8,128)S(1)}, u32[]{:S(2)}, u32[]{:S(2)}) collective-permute-start(f32[256,512]{1,0:T(8,128)S(1)} %get-tuple-element.29.far_ref), channel_id=1, source_target_pairs={{0,254},{1,255},{2,4},{3,5},{4,2},{5,3},{6,8},{7,9},{8,6},{9,7},{1... | collective-permute-start | bytes 1572872 | tf_op jit(solution)/shard_map/ppermute | solution.py:510
  13.1 12.6 %collective-permute-start.2 = (f32[64,128]{1,0:T(8,128)S(1)}, f32[64,128]{1,0:T(8,128)S(1)}, u32[]{:S(2)}, u32[]{:S(2)}) collective-permute-start(f32[64,128]{1,0:T(8,128)S(1)} %get-tuple-element.30), channel_id=1, source_target_pairs={{0,1},{1,0},{2,3},{3,2},{4,5},{5,4},{6,7},{7,6},{8,9},{9,8},{10,11... | collective-permute-start | bytes 98312 | tf_op jit(solution)/shard_map/ppermute | solution.py:510
  25.7 1.4 %collective-permute-start.6 = (f32[64,128]{1,0:T(8,128)S(1)}, f32[64,128]{1,0:T(8,128)S(1)}, u32[]{:S(2)}, u32[]{:S(2)}) collective-permute-start(f32[64,128]{1,0:T(8,128)S(1)} %collective-permute-done.2.side_ref), channel_id=1, source_target_pairs={{0,2},{1,3},{2,0},{3,1},{4,6},{5,7},{6,4},{7,5},{8,10},{9,11},{10,... | collective-permute-start | bytes 98312 | tf_op jit(solution)/shard_map/ppermute | solution.py:510
  27.1 4.0 %collective-permute-start.3 = (f32[64,128]{1,0:T(8,128)S(1)}, f32[64,128]{1,0:T(8,128)S(1)}, u32[]{:S(2)}, u32[]{:S(2)}) collective-permute-start(f32[64,128]{1,0:T(8,128)S(1)} %collective-permute-done.2.side_ref), channel_id=1, source_target_pairs={{0,254},{1,255},{2,4},{3,5},{4,2},{5,3},{6,8},{7,9},{8,6},{9,7},{1... | collective-permute-start | bytes 98312 | tf_op jit(solution)/shard_map/ppermute | solution.py:510
  39.2 6.9 %collective-permute-start.7 = (f32[48,128]{1,0:T(8,128)S(1)}, f32[48,128]{1,0:T(8,128)S(1)}, u32[]{:S(2)}, u32[]{:S(2)}) collective-permute-start(f32[48,128]{1,0:T(8,128)S(1)} %get-tuple-element.46), channel_id=1, source_target_pairs={{0,2},{2,0},{1,3},{3,1},{4,6},{6,4},{5,7},{7,5},{8,10},{10,8},{9,1... | collective-permute-start | bytes 73736 | tf_op jit(solution)/shard_map/ppermute | solution.py:459
  70.5 4.1 %collective-permute-start.8 = (f32[48,128]{1,0:T(8,128)S(1)}, f32[48,128]{1,0:T(8,128)S(1)}, u32[]{:S(2)}, u32[]{:S(2)}) collective-permute-start(f32[48,128]{1,0:T(8,128)S(1)} %reduce_sum.19.mine_ref), channel_id=1, source_target_pairs={{0,2},{2,0},{1,3},{3,1},{4,6},{6,4},{5,7},{7,5},{8,10},{10,8},{9,1... | collective-permute-start | bytes 73736 | tf_op jit(solution)/shard_map/ppermute | solution.py:466
